TPU v7x, 32 devices: a whole 2x2x4 slice. The times are simulated.
32 devices in a mesh: ctx: 16 (over z, y, core), head: 2 (over x).
Axes of the slice: x: 2, y: 2, z: 4, core: 2. Of those that a mesh axis runs over, the one named last changes fastest.
Arguments:
- queries: bfloat16 [16, 1024, 2048], P('ctx', None, 'head'), may hold values from -8 to 8
- keys: bfloat16 [16, 1024, 2048], P('ctx', None, 'head'), may hold values from -8 to 8
- values: bfloat16 [16, 1024, 2048], P('ctx', None, 'head'), may hold values from -24 to 24
- w_out: bfloat16 [2048, 4096], P('head'), may hold values from -0.125 to 0.125
Outputs:
- mixed: bfloat16 [16, 1024, 4096], P('ctx', 'head')
All inputs are finite; a program needn't handle non-finite values.
Results may differ from a plain program's by a relative error of at most 0.013.
Values may be sent and summed in bfloat16 or wider, within the bound.
A program may use at most 128 MiB of HBM per device.

v0:
```python
import jax
import jax.numpy as jnp
from jax import lax
from jax.sharding import PartitionSpec as P

HD = 128
GROUP = 4
masked_score = -1e30


def split_kinds(tensor, parity):
    groups = tensor.shape[2] // (2 * GROUP * HD)
    shaped = tensor.reshape((tensor.shape[0], tensor.shape[1], groups, 2, GROUP, HD))
    return shaped[:, :, :, parity].reshape((tensor.shape[0], tensor.shape[1], groups * GROUP, HD))


def normalized(scores):
    top = jnp.max(scores, axis=-1, keepdims=True)
    expo = jnp.exp(scores - top)
    total = jnp.sum(expo, axis=-1, keepdims=True)
    return (expo / total).astype(jnp.bfloat16)


def row_attention(queries, keys, values):
    scale = jnp.float32(1.0 / HD**0.5)
    length = queries.shape[1]
    causal = lax.broadcasted_iota(jnp.int32, (length, length), 1) <= lax.broadcasted_iota(
        jnp.int32, (length, length), 0
    )

    def one_row(triple):
        query_row, key_row, value_row = triple
        scores = (
            jnp.einsum("qhd,khd->hqk", query_row, key_row, preferred_element_type=jnp.float32)
            * scale
        )
        scores = jnp.where(causal, scores, masked_score)
        weights = normalized(scores)
        return jnp.einsum(
            "hqk,khd->qhd", weights, value_row, preferred_element_type=jnp.float32
        ).astype(jnp.bfloat16)

    return lax.map(one_row, (queries, keys, values))


def column_attention(triple):
    queries, keys, values = triple
    scale = jnp.float32(1.0 / HD**0.5)
    height = queries.shape[0]
    causal = lax.broadcasted_iota(jnp.int32, (height, height), 1) <= lax.broadcasted_iota(
        jnp.int32, (height, height), 0
    )
    scores = (
        jnp.einsum("rchd,schd->chrs", queries, keys, preferred_element_type=jnp.float32) * scale
    )
    scores = jnp.where(causal, scores, masked_score)
    weights = normalized(scores)
    attended = jnp.einsum(
        "chrs,schd->rchd", weights, values, preferred_element_type=jnp.float32
    ).astype(jnp.bfloat16)
    return lax.all_to_all(attended, "ctx", split_axis=0, concat_axis=1, tiled=True)


def on_device(queries, keys, values, w_out):
    rows_dev, stride, local_feat = queries.shape
    model_width = w_out.shape[1]
    groups = local_feat // (2 * GROUP * HD)
    row_out = row_attention(split_kinds(queries, 0), split_kinds(keys, 0), split_kinds(values, 0))
    col_triple = (split_kinds(queries, 1), split_kinds(keys, 1), split_kinds(values, 1))
    col_out = column_attention(
        (
            lax.all_to_all(col_triple[0], "ctx", split_axis=1, concat_axis=0, tiled=True),
            lax.all_to_all(col_triple[1], "ctx", split_axis=1, concat_axis=0, tiled=True),
            lax.all_to_all(col_triple[2], "ctx", split_axis=1, concat_axis=0, tiled=True),
        )
    )
    shaped = w_out.reshape((groups, 2, GROUP * HD, model_width))
    row_weights = shaped[:, 0].reshape((groups * GROUP * HD, model_width))
    col_weights = shaped[:, 1].reshape((groups * GROUP * HD, model_width))
    partial_value = jnp.dot(
        row_out.reshape((rows_dev * stride, -1)), row_weights, preferred_element_type=jnp.float32
    )
    partial_value = partial_value + jnp.dot(
        col_out.reshape((rows_dev * stride, -1)), col_weights, preferred_element_type=jnp.float32
    )
    partial_value = partial_value.reshape((rows_dev, stride, model_width))
    return lax.psum_scatter(
        partial_value.astype(jnp.bfloat16), "head", scatter_dimension=1, tiled=True
    )


def solution(mesh):
    return jax.shard_map(
        on_device,
        mesh=mesh,
        in_specs=(
            P("ctx", None, "head"),
            P("ctx", None, "head"),
            P("ctx", None, "head"),
            P("head", None),
        ),
        out_specs=P("ctx", "head", None),
        check_vma=False,
    )
```

profile of v0, /device:TPU:0, one launch (start us, length us, event | category | flops | bytes accessed | tf_op | source)
XLA Modules:
  0.0 254.6 jit_solution(13111694995554107261)
XLA Ops:
  6.5 2.9 %copy.35 = bf16[1,1024,1024]{1,2,0:T(8,128)(2,1)S(1)} copy(bf16[1,1024,1024]{2,1,0:T(8,128)(2,1)} %param.4) | data formatting | bytes 4194304 | tf_op args[0]
  9.4 0.0 copy-start
  9.4 0.1 slice_bitcast_fusion.6
  9.5 1.6 copy.41
  11.1 7.4 %all-to-all-start = ((bf16[1,1024,4,128]{3,2,0,1:T(4,128)(2,1)}), bf16[1,1024,4,128]{3,2,0,1:T(4,128)(2,1)S(1)}, u32[]{:S(2)}, u32[]{:S(2)}) async-start(bf16[1,1024,4,128]{3,2,0,1:T(4,128)(2,1)} %copy.41), calls=%async_computation | async-start | bytes 2097152 | tf_op jit(solution)/shard_map/all_to_all | solution.py:72
  18.5 4.0 %copy.37 = bf16[1,1024,1024]{1,2,0:T(8,128)(2,1)} copy(bf16[1,1024,1024]{2,1,0:T(8,128)(2,1)} %param.5) | data formatting | bytes 4194304 | tf_op args[1]
  22.5 0.0 copy-done
  22.5 1.3 slice_bitcast_fusion.5
  23.8 1.4 copy.43
  25.2 16.2 %all-to-all-done = bf16[1,1024,4,128]{3,2,0,1:T(4,128)(2,1)S(1)} async-done(((bf16[1,1024,4,128]{3,2,0,1:T(4,128)(2,1)}), bf16[1,1024,4,128]{3,2,0,1:T(4,128)(2,1)S(1)}, u32[]{:S(2)}, u32[]{:S(2)}) %all-to-all-start) | async-done | bytes 1048608 | tf_op jit(solution)/shard_map/all_to_all | solution.py:72
  41.4 6.8 %all-to-all-start.1 = ((bf16[1,1024,4,128]{3,2,0,1:T(4,128)(2,1)}), bf16[1,1024,4,128]{3,2,0,1:T(4,128)(2,1)}, u32[]{:S(2)}, u32[]{:S(2)}) async-start(bf16[1,1024,4,128]{3,2,0,1:T(4,128)(2,1)} %copy.43), calls=%async_computation.1 | async-start | bytes 2097152 | tf_op jit(solution)/shard_map/all_to_all | solution.py:73
  48.3 2.9 %copy.39 = bf16[1,1024,1024]{1,2,0:T(8,128)(2,1)S(1)} copy(bf16[1,1024,1024]{2,1,0:T(8,128)(2,1)} %param.6) | data formatting | bytes 4194304 | tf_op args[2]
  51.1 0.0 copy-done.1
  51.1 0.1 slice_bitcast_fusion.4
  51.2 1.5 copy.47
  52.7 18.5 %all-to-all-done.1 = bf16[1,1024,4,128]{3,2,0,1:T(4,128)(2,1)} async-done(((bf16[1,1024,4,128]{3,2,0,1:T(4,128)(2,1)}), bf16[1,1024,4,128]{3,2,0,1:T(4,128)(2,1)}, u32[]{:S(2)}, u32[]{:S(2)}) %all-to-all-start.1) | async-done | bytes 1048608 | tf_op jit(solution)/shard_map/all_to_all | solution.py:73
  71.2 6.8 %all-to-all-start.2 = ((bf16[1,1024,4,128]{3,2,0,1:T(4,128)(2,1)}), bf16[1,1024,4,128]{3,2,0,1:T(4,128)(2,1)}, u32[]{:S(2)}, u32[]{:S(2)}) async-start(bf16[1,1024,4,128]{3,2,0,1:T(4,128)(2,1)} %copy.47), calls=%async_computation.2 | async-start | bytes 2097152 | tf_op jit(solution)/shard_map/all_to_all | solution.py:74
  78.1 1.3 iota_compare_fusion
  79.4 11.8 %fusion.29 = (f32[4,1024]{1,0:T(4,128)S(1)}, f32[4,1024,1024]{1,2,0:T(8,128)}) fusion(pred[1024,1024]{0,1:T(8,128)(4,1)} %iota_compare_fusion, bf16[1,1024,1,2,4,128]{1,5,4,3,2,0:T(8,128)(2,1)} %bitcast.62, bf16[1,1024,1,2,4,128]{1,5,4,3,2,0:T(8,128)(2,1)} %bitcast.64), kind=kOutput, calls=%fused_computation.46 | convolution fusion | flops 1090520064 | bytes 19939328 | tf_op jit(solution)/shard_map/while/body/eval_jaxpr/sub | solution.py:19
  91.2 0.0 copy-done.2
  91.2 4.6 %fusion.30 = (f32[64,4,16]{2,1,0:T(4,128)S(1)}, f32[64,4,16,16]{2,3,1,0:T(8,128)}) fusion(pred[16,16]{0,1:T(8,128)(4,1)S(1)} %iota_compare_fusion.1, bf16[16,64,4,128]{3,2,1,0:T(4,128)(2,1)} %bitcast.13, bf16[16,64,4,128]{3,2,1,0:T(4,128)(2,1)S(1)} %bitcast.65), kind=kOutput, calls=%fused_computation.47 | convolution fusion | flops 17039376 | bytes 2375936 | tf_op jit(solution)/shard_map/sub | solution.py:19
  95.8 5.2 %all-to-all-done.2 = bf16[1,1024,4,128]{3,2,0,1:T(4,128)(2,1)} async-done(((bf16[1,1024,4,128]{3,2,0,1:T(4,128)(2,1)}), bf16[1,1024,4,128]{3,2,0,1:T(4,128)(2,1)}, u32[]{:S(2)}, u32[]{:S(2)}) %all-to-all-start.2) | async-done | bytes 1048608 | tf_op jit(solution)/shard_map/all_to_all | solution.py:74
  101.0 2.7 %fusion.13 = bf16[16,64,4,128]{3,0,2,1:T(8,128)(2,1)S(1)} fusion(f32[64,4,16,16]{2,3,1,0:T(8,128)} %get-tuple-element.24, bf16[16,64,4,128]{3,2,1,0:T(4,128)(2,1)} %bitcast.15, f32[64,4,16]{2,1,0:T(4,128)S(1)} %get-tuple-element.17), kind=kOutput, calls=%fused_computation.23 | convolution fusion | flops 17432576 | bytes 2375680 | tf_op jit(solution)/shard_map/chrs,schd->rchd/dot_general | solution.py:58
  103.7 1.5 copy.51
  105.2 6.8 %all-to-all-start.3 = ((bf16[16,64,4,128]{3,2,1,0:T(4,128)(2,1)}), bf16[16,64,4,128]{3,2,1,0:T(4,128)(2,1)S(1)}, u32[]{:S(2)}, u32[]{:S(2)}) async-start(bf16[16,64,4,128]{3,2,1,0:T(4,128)(2,1)} %copy.51), calls=%async_computation.3 | async-start | bytes 2097152 | tf_op jit(solution)/shard_map/all_to_all | solution.py:61
  112.0 0.2 reduce-scatter.2.cloned.1.call-start
  112.2 7.1 %fusion.12 = bf16[4,1024,128]{1,2,0:T(8,128)(2,1)S(1)} fusion(f32[4,1024,1024]{1,2,0:T(8,128)} %get-tuple-element.16, f32[4,1024]{1,0:T(4,128)S(1)} %get-tuple-element.15, bf16[1,1024,1,2,4,128]{1,5,4,3,2,0:T(8,128)(2,1)S(1)} %bitcast.60), kind=kOutput, calls=%fused_computation.21 | convolution fusion | flops 1082654720 | bytes 18890752 | tf_op jit(solution)/shard_map/while/body/eval_jaxpr/hqk,khd->qhd/dot_general | solution.py:39
  119.3 10.3 %fusion.8 = f32[1024,4096]{1,0:T(8,128)} fusion(bf16[1024,512]{0,1:T(8,128)(2,1)S(1)} %bitcast.69, bf16[1,2,512,4096]{3,2,1,0:T(8,128)(2,1)} %bitcast.67), kind=kOutput, calls=%fused_computation.14 | convolution fusion | flops 4294967296 | bytes 22020096 | tf_op jit(solution)/shard_map/dot_general | solution.py:80
  129.6 5.3 %all-to-all-done.3 = bf16[16,64,4,128]{3,2,1,0:T(4,128)(2,1)S(1)} async-done(((bf16[16,64,4,128]{3,2,1,0:T(4,128)(2,1)}), bf16[16,64,4,128]{3,2,1,0:T(4,128)(2,1)S(1)}, u32[]{:S(2)}, u32[]{:S(2)}) %all-to-all-start.3) | async-done | bytes 1048608 | tf_op jit(solution)/shard_map/all_to_all | solution.py:61
  134.9 11.3 %fusion.3 = bf16[1,1024,4096]{2,1,0:T(8,128)(2,1)} fusion(f32[1024,4096]{1,0:T(8,128)} %fusion.8, bf16[1,2,512,4096]{3,2,1,0:T(8,128)(2,1)} %bitcast.68, bf16[128,8,4,128]{3,2,1,0:T(4,128)(2,1)S(1)} %bitcast.66), kind=kOutput, calls=%fused_computation.7 | convolution fusion | flops 4303355904 | bytes 30408704 | tf_op jit(solution)/shard_map/dot_general | solution.py:83
  146.2 0.0 reduce-scatter.2.cloned.1.call-update
  146.2 101.6 %reduce-scatter.2.cloned.1.call-done = bf16[1,512,4096]{2,1,0:T(8,128)(2,1)} async-done(((bf16[1,1024,4096]{2,1,0:T(8,128)(2,1)}), bf16[1,512,4096]{2,1,0:T(8,128)(2,1)}) %reduce-scatter.2.cloned.1.call-update) | async-done | bytes 4194320 | tf_op jit(solution)/shard_map/reduce_scatter | solution.py:87
  (3 shorter events, 0.0 us)
Async XLA Ops:
  9.4 13.1 %copy-start = (bf16[1,1024,1024]{1,2,0:T(8,128)(2,1)}, bf16[1,1024,1024]{1,2,0:T(8,128)(2,1)S(1)}, u32[]{:S(2)}) copy-start(bf16[1,1024,1024]{1,2,0:T(8,128)(2,1)S(1)} %copy.35) | copy-start | bytes 6291460
  11.1 30.3 %all-to-all-start = ((bf16[1,1024,4,128]{3,2,0,1:T(4,128)(2,1)}), bf16[1,1024,4,128]{3,2,0,1:T(4,128)(2,1)S(1)}, u32[]{:S(2)}, u32[]{:S(2)}) async-start(bf16[1,1024,4,128]{3,2,0,1:T(4,128)(2,1)} %copy.41), calls=%async_computation | async-start | bytes 2097152 | tf_op jit(solution)/shard_map/all_to_all | solution.py:72
  41.4 9.7 %copy-start.1 = (bf16[1,1024,4,128]{3,2,0,1:T(4,128)(2,1)}, bf16[1,1024,4,128]{3,2,0,1:T(4,128)(2,1)S(1)}, u32[]{:S(2)}) copy-start(bf16[1,1024,4,128]{3,2,0,1:T(4,128)(2,1)S(1)} %all-to-all-done) | copy-start | bytes 3145732
  41.4 29.8 %all-to-all-start.1 = ((bf16[1,1024,4,128]{3,2,0,1:T(4,128)(2,1)}), bf16[1,1024,4,128]{3,2,0,1:T(4,128)(2,1)}, u32[]{:S(2)}, u32[]{:S(2)}) async-start(bf16[1,1024,4,128]{3,2,0,1:T(4,128)(2,1)} %copy.43), calls=%async_computation.1 | async-start | bytes 2097152 | tf_op jit(solution)/shard_map/all_to_all | solution.py:73
  71.2 29.8 %all-to-all-start.2 = ((bf16[1,1024,4,128]{3,2,0,1:T(4,128)(2,1)}), bf16[1,1024,4,128]{3,2,0,1:T(4,128)(2,1)}, u32[]{:S(2)}, u32[]{:S(2)}) async-start(bf16[1,1024,4,128]{3,2,0,1:T(4,128)(2,1)} %copy.47), calls=%async_computation.2 | async-start | bytes 2097152 | tf_op jit(solution)/shard_map/all_to_all | solution.py:74
  79.4 11.8 %copy-start.2 = (bf16[1,1024,4,128]{3,2,0,1:T(4,128)(2,1)S(1)}, bf16[1,1024,4,128]{3,2,0,1:T(4,128)(2,1)}, u32[]{:S(2)}) copy-start(bf16[1,1024,4,128]{3,2,0,1:T(4,128)(2,1)} %copy-done.1) | copy-start | bytes 3145732
  105.2 29.7 %all-to-all-start.3 = ((bf16[16,64,4,128]{3,2,1,0:T(4,128)(2,1)}), bf16[16,64,4,128]{3,2,1,0:T(4,128)(2,1)S(1)}, u32[]{:S(2)}, u32[]{:S(2)}) async-start(bf16[16,64,4,128]{3,2,1,0:T(4,128)(2,1)} %copy.51), calls=%async_computation.3 | async-start | bytes 2097152 | tf_op jit(solution)/shard_map/all_to_all | solution.py:61
  112.0 135.8 %reduce-scatter.2.cloned.1.call-start = ((), (), s32[]{:S(2)}) async-start(), calls=%async_computation.5 | async-start | bytes 12582912 | tf_op jit(solution)/shard_map/reduce_scatter | solution.py:87
Sparse Core Ops, SparseCore 0:
  146.3 101.4 reduce-scatter.1
where the time goes:
time: 255 us
  waiting for transfers between devices  147 us (58%)
  matrix products  47.8 us (19%)
  starting transfers between devices  28.1 us (11%)
  local copies, waits for them, and re-layouts  17.1 us (7%)
  between operations  13.5 us (5%)
    reduce_scatter x1, waiting for transfers between devices, on_device(): lax.psum_scatter(partial_value.astype(jnp.bfloat16), 'head', scatter_dime...  102 us
    all_to_all x1, waiting for transfers between devices, on_device(): lax.all_to_all(col_triple[1], 'ctx', split_axis=1, concat_axis=0, tiled=T...  18.5 us
    sub x2, matrix products, normalized(): expo = jnp.exp(scores - top)  16.4 us
    all_to_all x1, waiting for transfers between devices, on_device(): lax.all_to_all(col_triple[0], 'ctx', split_axis=1, concat_axis=0, tiled=T...  16.2 us
    dot_general x1, matrix products, on_device(): jnp.dot(col_out.reshape((rows_dev * stride, -1)), col_weights, preferred_...  11.3 us
    dot_general x1, matrix products, on_device(): jnp.dot(row_out.reshape((rows_dev * stride, -1)), row_weights, preferred_...  10.3 us
    unnamed x9, local copies, waits for them, and re-layouts  9.69 us
    all_to_all x1, starting transfers between devices, on_device(): lax.all_to_all(col_triple[0], 'ctx', split_axis=1, concat_axis=0, tiled=T...  7.41 us
  transfers between devices with their start and end apart: 5, of which 5 were waited for; matrix products, arithmetic and copies ran while one was open for 18% of the time, Pallas kernels for 0%

commit v1 on v0

--- a/solution.py
+++ b/solution.py
@@ -67,10 +67,19 @@
     groups = local_feat // (2 * GROUP * HD)
     row_out = row_attention(split_kinds(queries, 0), split_kinds(keys, 0), split_kinds(values, 0))
     col_triple = (split_kinds(queries, 1), split_kinds(keys, 1), split_kinds(values, 1))
+    shifts_all_lift = lambda arr, chip_axis: jnp.concatenate(
+        lax.all_to_all(
+            jnp.stack(jnp.split(arr, lax.axis_size(chip_axis), axis=1)),
+            axis_name=chip_axis,
+            split_axis=0,
+            concat_axis=0,
+        ),
+        axis=0,
+    )
     col_out = column_attention(
         (
             lax.all_to_all(col_triple[0], "ctx", split_axis=1, concat_axis=0, tiled=True),
-            lax.all_to_all(col_triple[1], "ctx", split_axis=1, concat_axis=0, tiled=True),
+            shifts_all_lift(col_triple[1], "ctx"),
             lax.all_to_all(col_triple[2], "ctx", split_axis=1, concat_axis=0, tiled=True),
         )
     )

time: 255 us -> 275 us (1.078)
  local copies, waits for them, and re-layouts: 17.1 us -> 55.2 us
  waiting for transfers between devices: 147 us -> 130 us
    split x0 -> x17, local copies, waits for them, and re-layouts: none -> 23.6 us  [on_device(): jnp.split(arr, lax.axis_size(chip_axis), axis=1)]
    all_to_all x1, waiting for transfers between devices: 16.2 us -> 0.01 us  [on_device(): lax.all_to_all(col_triple[0], 'ctx', split_axis=1, concat_axis=0, tiled=T...]
    unnamed x9 -> x24, local copies, waits for them, and re-layouts: 9.69 us -> 21.9 us
    another operation x6 -> x5, local copies, waits for them, and re-layouts: 5.93 us -> 5.59 us  [split_kinds(): shaped[:, :, :, parity]]
  transfers between devices with their start and end apart: 5 -> 5, of which waited for: 5 -> 4; matrix products, arithmetic and copies ran while one was open for 18% -> 30% of each run, Pallas kernels for 0% -> 0%
where the time goes in v1:
time: 275 us; the launch traced here: 273 us
  waiting for transfers between devices  130 us (47%)
  local copies, waits for them, and re-layouts  55.2 us (20%)
  matrix products  45.7 us (17%)
  starting transfers between devices  27.4 us (10%)
  between operations  13.5 us (5%)
    reduce_scatter x1, waiting for transfers between devices, on_device(): lax.psum_scatter(partial_value.astype(jnp.bfloat16), 'head', scatter_dime...  102 us
    split x17, local copies, waits for them, and re-layouts, on_device(): jnp.split(arr, lax.axis_size(chip_axis), axis=1)  23.6 us
    unnamed x24, local copies, waits for them, and re-layouts  21.9 us
    all_to_all x1, waiting for transfers between devices, on_device(): lax.all_to_all(jnp.stack(jnp.split(arr, lax.axis_size(chip_axis), axis=1)...  16.2 us
    sub x2, matrix products, normalized(): expo = jnp.exp(scores - top)  14.9 us
    dot_general x1, matrix products, on_device(): jnp.dot(col_out.reshape((rows_dev * stride, -1)), col_weights, preferred_...  11.3 us
    dot_general x1, matrix products, on_device(): jnp.dot(row_out.reshape((rows_dev * stride, -1)), row_weights, preferred_...  10.3 us
    all_to_all x1, starting transfers between devices, on_device(): lax.all_to_all(col_triple[0], 'ctx', split_axis=1, concat_axis=0, tiled=T...  7.41 us
  transfers between devices with their start and end apart: 5, of which 4 were waited for; matrix products, arithmetic and copies ran while one was open for 30% of the time, Pallas kernels for 0%

profile of v1, /device:TPU:0, one launch (start us, length us, event | category | flops | bytes accessed | tf_op | source)
XLA Modules:
  0.0 272.9 jit_solution(15023224479432862639)
XLA Ops:
  6.5 2.9 %copy.621 = bf16[1,1024,1024]{1,2,0:T(8,128)(2,1)S(1)} copy(bf16[1,1024,1024]{2,1,0:T(8,128)(2,1)} %param.4) | data formatting | bytes 4194304 | tf_op args[0]
  10.9 7.4 %all-to-all-start.1 = ((bf16[1,1024,4,128]{3,2,0,1:T(4,128)(2,1)}), bf16[1,1024,4,128]{3,2,0,1:T(4,128)(2,1)S(1)}, u32[]{:S(2)}, u32[]{:S(2)}) async-start(bf16[1,1024,4,128]{3,2,0,1:T(4,128)(2,1)} %copy.645), calls=%async_computation.1 | async-start | bytes 2097152 | tf_op jit(solution)/shard_map/all_to_all | solution.py:81
  18.3 3.9 %copy.623 = bf16[1,1024,1024]{1,2,0:T(8,128)(2,1)} copy(bf16[1,1024,1024]{2,1,0:T(8,128)(2,1)} %param.5) | data formatting | bytes 4194304 | tf_op args[1]
  23.6 1.6 fusion.30
  25.2 1.6 copy.642
  26.8 1.6 copy.641
  28.4 1.6 copy.640
  30.1 1.6 copy.639
  31.7 1.6 copy.638
  33.3 1.6 copy.637
  34.9 1.6 copy.636
  36.5 1.6 copy.635
  38.2 1.6 copy.634
  39.8 1.6 copy.633
  41.4 1.6 copy.632
  43.0 1.6 copy.631
  44.6 1.6 copy.630
  59.2 1.9 copy.643
  61.1 6.1 %all-to-all-start = ((bf16[16,1,64,4,128]{4,3,2,1,0:T(4,128)(2,1)}), bf16[16,1,64,4,128]{4,3,2,1,0:T(4,128)(2,1)}, u32[]{:S(2)}, u32[]{:S(2)}) async-start(bf16[16,1,64,4,128]{4,3,2,1,0:T(4,128)(2,1)} %copy.643), calls=%async_computation | async-start | bytes 2097152 | tf_op jit(solution)/shard_map/all_to_all | solution.py:71
  67.1 4.0 %copy.625 = bf16[1,1024,1024]{1,2,0:T(8,128)(2,1)} copy(bf16[1,1024,1024]{2,1,0:T(8,128)(2,1)} %param.6) | data formatting | bytes 4194304 | tf_op args[2]
  73.9 16.2 %all-to-all-done = bf16[16,1,64,4,128]{4,3,2,1,0:T(4,128)(2,1)} async-done(((bf16[16,1,64,4,128]{4,3,2,1,0:T(4,128)(2,1)}), bf16[16,1,64,4,128]{4,3,2,1,0:T(4,128)(2,1)}, u32[]{:S(2)}, u32[]{:S(2)}) %all-to-all-start) | async-done | bytes 1048608 | tf_op jit(solution)/shard_map/all_to_all | solution.py:71
  90.1 6.9 %all-to-all-start.2 = ((bf16[1,1024,4,128]{3,2,0,1:T(4,128)(2,1)}), bf16[1,1024,4,128]{3,2,0,1:T(4,128)(2,1)}, u32[]{:S(2)}, u32[]{:S(2)}) async-start(bf16[1,1024,4,128]{3,2,0,1:T(4,128)(2,1)} %copy.648), calls=%async_computation.2 | async-start | bytes 2097152 | tf_op jit(solution)/shard_map/all_to_all | solution.py:83
  98.3 11.6 %fusion.31 = (f32[4,1024]{1,0:T(4,128)S(1)}, f32[4,1024,1024]{1,2,0:T(8,128)}) fusion(pred[1024,1024]{0,1:T(8,128)(4,1)} %iota_compare_fusion, bf16[1,1024,1,2,4,128]{1,5,4,3,2,0:T(8,128)(2,1)S(1)} %bitcast.105, bf16[1,1024,1,2,4,128]{1,5,4,3,2,0:T(8,128)(2,1)} %bitcast.107), kind=kOutput, calls=%fused_computation.64 | convolution fusion | flops 1090520064 | bytes 19939328 | tf_op jit(solution)/shard_map/while/body/eval_jaxpr/sub | solution.py:19
  109.9 3.3 %fusion.32 = (f32[64,4,16]{2,1,0:T(4,128)S(1)}, f32[64,4,16,16]{2,3,1,0:T(8,128)S(1)}) fusion(pred[16,16]{0,1:T(8,128)(4,1)S(1)} %iota_compare_fusion.1, bf16[16,64,4,128]{3,2,1,0:T(4,128)(2,1)S(1)} %bitcast.110, bf16[16,1,64,4,128]{4,3,2,1,0:T(4,128)(2,1)} %all-to-all-done), kind=kOutput, calls=%fused_computation.65 | convolution fusion | flops 17039376 | bytes 2375936 | tf_op jit(solution)/shard_map/sub | solution.py:19
  113.2 6.7 %all-to-all-done.2 = bf16[1,1024,4,128]{3,2,0,1:T(4,128)(2,1)} async-done(((bf16[1,1024,4,128]{3,2,0,1:T(4,128)(2,1)}), bf16[1,1024,4,128]{3,2,0,1:T(4,128)(2,1)}, u32[]{:S(2)}, u32[]{:S(2)}) %all-to-all-start.2) | async-done | bytes 1048608 | tf_op jit(solution)/shard_map/all_to_all | solution.py:83
  119.9 2.1 fusion.13
  123.4 6.8 %all-to-all-start.3 = ((bf16[16,64,4,128]{3,2,1,0:T(4,128)(2,1)}), bf16[16,64,4,128]{3,2,1,0:T(4,128)(2,1)S(1)}, u32[]{:S(2)}, u32[]{:S(2)}) async-start(bf16[16,64,4,128]{3,2,1,0:T(4,128)(2,1)} %copy.652), calls=%async_computation.3 | async-start | bytes 2097152 | tf_op jit(solution)/shard_map/all_to_all | solution.py:61
  130.5 7.1 %fusion.12 = bf16[4,1024,128]{1,2,0:T(8,128)(2,1)S(1)} fusion(f32[4,1024,1024]{1,2,0:T(8,128)} %get-tuple-element.40, f32[4,1024]{1,0:T(4,128)S(1)} %get-tuple-element.39, bf16[1,1024,1,2,4,128]{1,5,4,3,2,0:T(8,128)(2,1)S(1)} %bitcast.109), kind=kOutput, calls=%fused_computation.21 | convolution fusion | flops 1082654720 | bytes 18890752 | tf_op jit(solution)/shard_map/while/body/eval_jaxpr/hqk,khd->qhd/dot_general | solution.py:39
  137.6 10.3 %fusion.8 = f32[1024,4096]{1,0:T(8,128)} fusion(bf16[1024,512]{0,1:T(8,128)(2,1)S(1)} %bitcast.114, bf16[1,2,512,4096]{3,2,1,0:T(8,128)(2,1)} %bitcast.112), kind=kOutput, calls=%fused_computation.14 | convolution fusion | flops 4294967296 | bytes 22020096 | tf_op jit(solution)/shard_map/dot_general | solution.py:89
  147.9 5.2 %all-to-all-done.3 = bf16[16,64,4,128]{3,2,1,0:T(4,128)(2,1)S(1)} async-done(((bf16[16,64,4,128]{3,2,1,0:T(4,128)(2,1)}), bf16[16,64,4,128]{3,2,1,0:T(4,128)(2,1)S(1)}, u32[]{:S(2)}, u32[]{:S(2)}) %all-to-all-start.3) | async-done | bytes 1048608 | tf_op jit(solution)/shard_map/all_to_all | solution.py:61
  153.1 11.3 %fusion.3 = bf16[1,1024,4096]{2,1,0:T(8,128)(2,1)} fusion(f32[1024,4096]{1,0:T(8,128)} %fusion.8, bf16[1,2,512,4096]{3,2,1,0:T(8,128)(2,1)} %bitcast.113, bf16[128,8,4,128]{3,2,1,0:T(4,128)(2,1)S(1)} %bitcast.111), kind=kOutput, calls=%fused_computation.7 | convolution fusion | flops 4303355904 | bytes 30408704 | tf_op jit(solution)/shard_map/dot_general | solution.py:92
  164.4 101.6 %reduce-scatter.2.cloned.1.call-done = bf16[1,512,4096]{2,1,0:T(8,128)(2,1)} async-done(((bf16[1,1024,4096]{2,1,0:T(8,128)(2,1)}), bf16[1,512,4096]{2,1,0:T(8,128)(2,1)}) %reduce-scatter.2.cloned.1.call-update) | async-done | bytes 4194320 | tf_op jit(solution)/shard_map/reduce_scatter | solution.py:96
  (36 shorter events, 21.6 us)
Async XLA Ops:
  10.9 50.2 %all-to-all-start.1 = ((bf16[1,1024,4,128]{3,2,0,1:T(4,128)(2,1)}), bf16[1,1024,4,128]{3,2,0,1:T(4,128)(2,1)S(1)}, u32[]{:S(2)}, u32[]{:S(2)}) async-start(bf16[1,1024,4,128]{3,2,0,1:T(4,128)(2,1)} %copy.645), calls=%async_computation.1 | async-start | bytes 2097152 | tf_op jit(solution)/shard_map/all_to_all | solution.py:81
  61.1 10.0 %copy-start.1 = (bf16[1,1024,4,128]{3,2,0,1:T(4,128)(2,1)}, bf16[1,1024,4,128]{3,2,0,1:T(4,128)(2,1)S(1)}, u32[]{:S(2)}) copy-start(bf16[1,1024,4,128]{3,2,0,1:T(4,128)(2,1)S(1)} %all-to-all-done.1) | copy-start | bytes 3145732
  61.1 29.0 %all-to-all-start = ((bf16[16,1,64,4,128]{4,3,2,1,0:T(4,128)(2,1)}), bf16[16,1,64,4,128]{4,3,2,1,0:T(4,128)(2,1)}, u32[]{:S(2)}, u32[]{:S(2)}) async-start(bf16[16,1,64,4,128]{4,3,2,1,0:T(4,128)(2,1)} %copy.643), calls=%async_computation | async-start | bytes 2097152 | tf_op jit(solution)/shard_map/all_to_all | solution.py:71
  90.1 29.8 %all-to-all-start.2 = ((bf16[1,1024,4,128]{3,2,0,1:T(4,128)(2,1)}), bf16[1,1024,4,128]{3,2,0,1:T(4,128)(2,1)}, u32[]{:S(2)}, u32[]{:S(2)}) async-start(bf16[1,1024,4,128]{3,2,0,1:T(4,128)(2,1)} %copy.648), calls=%async_computation.2 | async-start | bytes 2097152 | tf_op jit(solution)/shard_map/all_to_all | solution.py:83
  98.3 11.6 %copy-start.2 = (bf16[1,1024,4,128]{3,2,0,1:T(4,128)(2,1)S(1)}, bf16[1,1024,4,128]{3,2,0,1:T(4,128)(2,1)}, u32[]{:S(2)}) copy-start(bf16[1,1024,4,128]{3,2,0,1:T(4,128)(2,1)} %copy-done.1) | copy-start | bytes 3145732
  122.0 8.5 %copy-start = (bf16[1,1024,1024]{1,2,0:T(8,128)(2,1)S(1)}, bf16[1,1024,1024]{1,2,0:T(8,128)(2,1)}, u32[]{:S(2)}) copy-start(bf16[1,1024,1024]{1,2,0:T(8,128)(2,1)} %copy.625) | copy-start | bytes 6291460
  123.4 29.7 %all-to-all-start.3 = ((bf16[16,64,4,128]{3,2,1,0:T(4,128)(2,1)}), bf16[16,64,4,128]{3,2,1,0:T(4,128)(2,1)S(1)}, u32[]{:S(2)}, u32[]{:S(2)}) async-start(bf16[16,64,4,128]{3,2,1,0:T(4,128)(2,1)} %copy.652), calls=%async_computation.3 | async-start | bytes 2097152 | tf_op jit(solution)/shard_map/all_to_all | solution.py:61
  130.2 135.8 %reduce-scatter.2.cloned.1.call-start = ((), (), s32[]{:S(2)}) async-start(), calls=%async_computation.5 | async-start | bytes 12582912 | tf_op jit(solution)/shard_map/reduce_scatter | solution.py:96
Sparse Core Ops, SparseCore 0:
  164.6 101.4 reduce-scatter.1
